TPU v7x, 32 devices: a whole 2x2x4 slice. The times are simulated.
32 devices in a mesh: ens: 4 (over y, x), lon: 8 (over z, core).
Axes of the slice: x: 2, y: 2, z: 4, core: 2. Of those that a mesh axis runs over, the one named last changes fastest.
Arguments:
- control: float32 [8, 1024, 512], P('ens', None, 'lon'), may hold values from -6 to 6
- residual: float32 [8, 1024, 512], P('ens', None, 'lon'), may hold values from -6 to 6
- direction: float32 [8, 1024, 512], P('ens', None, 'lon'), may hold values from -6 to 6
- ens_perturb: bfloat16 [8, 3, 1024, 512], P('ens', None, None, 'lon'), may hold values from -1.5 to 1.5
- localize: float32 [1024, 1024], replicated, may hold values from -0.5 to 1.5
- obs_cell: int32 [32768], P('lon'), may hold values from 0 to 65535
- obs_slot: int32 [32768], P('lon'), may hold values from 0 to 3
- obs_weight: float32 [32768], P('lon'), may hold values from 0.5 to 4
Outputs:
- control_new: float32 [8, 1024, 512], P('ens', None, 'lon')
- residual_new: float32 [8, 1024, 512], P('ens', None, 'lon')
- direction_new: float32 [8, 1024, 512], P('ens', None, 'lon')
Inputs may be any that keep to these rules, and one draw needn't show every extreme that they name: `obs_cell`: row-major cell within the entry's own longitude tile: row times 64 plus column. `obs_slot`: slot n < 3 observes the height after model step n + 1; slot 3 marks a padding entry that observes nothing.
All inputs are finite; a program needn't handle non-finite values.
Results may differ from a plain program's by a relative error of at most 0.0003.
Values sent between devices are 32-bit elements; how exact they have to be, the bound alone decides.
A program may use at most 64 MiB of HBM per device.

v0:
```python
import jax
import jax.numpy as jnp
from jax import lax
from jax.sharding import PartitionSpec as P

STEPS = 3


wave_speed = 0.35
rotation = 0.2


def extended(block, sides, width):
    for axis, dim in sides:
        count = lax.axis_size(axis)
        forward = [(i, i + 1) for i in range(count - 1)]
        forward.append((count - 1, 0))
        backward = [(target, source) for source, target in forward]
        low = lax.ppermute(
            lax.slice_in_dim(block, block.shape[dim] - width, None, axis=dim), axis, forward
        )
        high = lax.ppermute(lax.slice_in_dim(block, 0, width, axis=dim), axis, backward)
        block = jnp.concatenate([low, block, high], axis=dim)
    return block


def grid_factors(row_ids, lat_total):
    latitude = (-1.0 / 3.0 + 2.0 / 3.0 * (row_ids + 0.5) / lat_total) * jnp.pi
    return (1.0 / jnp.cos(latitude), jnp.sin(latitude))


def model_step(fields, orient, metric, coriolis):
    lon_wide = extended(fields, (("lon", 2),), 1)
    lat_wide = jnp.pad(fields, ((0, 0), (1, 1), (0, 0)))
    lon_diff = 0.5 * metric[:, None] * (lon_wide[:, :, 2:] - lon_wide[:, :, :-2])
    lat_diff = 0.5 * (lat_wide[:, 2:] - lat_wide[:, :-2])
    height, zonal, meridional = (fields[0], fields[1], fields[2])
    speed = orient * wave_speed
    turning = orient * rotation * coriolis[:, None]
    return jnp.stack(
        [
            height - speed * (lon_diff[1] + lat_diff[2]),
            zonal - speed * lon_diff[0] + turning * meridional,
            meridional - speed * lat_diff[0] - turning * zonal,
        ]
    )


def body(control, residual, direction, ens_perturb, localize, obs_cell, obs_slot, obs_weight):
    hi = lax.Precision.HIGHEST
    lat_total = localize.shape[0]
    tile_cols = control.shape[2]
    localized = jnp.einsum("ij,mjc->mic", localize, direction, precision=hi)
    increment = jnp.sum(ens_perturb.astype(jnp.float32) * localized[:, None], axis=0)
    lat_slab = lax.psum(increment, "ens")
    slab_rows = lat_slab.shape[1]
    cells = slab_rows * tile_cols
    row_ids = jnp.arange(slab_rows, dtype=jnp.int32).astype(jnp.float32)
    metric, coriolis = grid_factors(row_ids, lat_total)
    local_row = obs_cell // tile_cols
    inside = (local_row >= 0) & (local_row < slab_rows) & (obs_slot < STEPS)
    cell_index = jnp.clip(local_row, 0, slab_rows - 1) * tile_cols + obs_cell % tile_cols
    slot_index = obs_slot * cells + cell_index
    gather_index = jnp.clip(slot_index, 0, STEPS * cells - 1)
    tl_state = lat_slab
    heights = []
    for moment in range(STEPS):
        tl_state = model_step(tl_state, 1.0, metric, coriolis)
        heights.append(tl_state[0].reshape(-1))
    observed = jnp.concatenate(heights)[gather_index]
    weighted = jnp.where(inside, obs_weight * observed, 0.0)
    forcing = jnp.zeros(((STEPS + 1) * cells,), jnp.float32).at[slot_index].add(weighted)
    forcing = forcing.reshape(STEPS + 1, slab_rows, tile_cols)
    adjoint = jnp.zeros(lat_slab.shape, jnp.float32)
    for moment in reversed(range(STEPS)):
        adjoint = adjoint.at[0].add(forcing[moment])
        adjoint = model_step(adjoint, -1.0, metric, coriolis)
    projected = jnp.sum(ens_perturb.astype(jnp.float32) * adjoint[None], axis=1)
    pulled_back = jnp.einsum("ji,mjc->mic", localize, projected, precision=hi)
    image_vec = direction + pulled_back
    norm_old, curvature, cross_term, square = lax.psum(
        (
            jnp.sum(residual * residual),
            jnp.sum(direction * image_vec),
            jnp.sum(residual * image_vec),
            jnp.sum(image_vec * image_vec),
        ),
        ("ens", "lon"),
    )
    step_size = norm_old / curvature
    control_new = control + step_size * direction
    residual_new = residual - step_size * image_vec
    norm_new = norm_old - 2.0 * step_size * cross_term + step_size * step_size * square
    direction_new = residual_new + norm_new / norm_old * direction
    return (control_new, residual_new, direction_new)


def solution(mesh):
    in_specs = (
        P("ens", None, "lon"),
        P("ens", None, "lon"),
        P("ens", None, "lon"),
        P("ens", None, None, "lon"),
        P(),
        P("lon"),
        P("lon"),
        P("lon"),
    )
    out_specs = (P("ens", None, "lon"), P("ens", None, "lon"), P("ens", None, "lon"))
    return jax.shard_map(body, mesh=mesh, in_specs=in_specs, out_specs=out_specs, check_vma=False)
```

profile of v0, /device:TPU:0, one launch (start us, length us, event | category | flops | bytes accessed | tf_op | source)
XLA Modules:
  0.0 209.6 jit_solution(16358781422589472048)
XLA Ops:
  7.2 6.8 %fusion.6 = f32[2,1024,64]{1,2,0:T(8,128)S(1)} fusion(f32[2,1024,64]{1,2,0:T(8,128)} %param.16, f32[1024,1024]{1,0:T(8,128)} %param.18), kind=kOutput, calls=%fused_computation.10 | convolution fusion | flops 1610612736 | bytes 5242880 | tf_op jit(solution)/shard_map/ij,mjc->mic/dot_general | solution.py:53
  14.1 1.1 fusion.4
  15.3 51.4 %all-reduce.10.cloned.1.call-done = f32[3,1024,64]{1,2,0:T(8,128)} async-done(((f32[3,1024,64]{1,2,0:T(8,128)}), f32[3,1024,64]{1,2,0:T(8,128)}) %all-reduce.10.cloned.1.call-update) | async-done | bytes 786448 | tf_op jit(solution)/shard_map/psum | solution.py:55
  66.7 1.0 fusion.89
  67.7 2.7 %collective-permute-start = (f32[3,1024,1]{1,2,0:T(1,128)S(1)}, f32[3,1024,1]{1,2,0:T(1,128)S(1)}, u32[]{:S(2)}, u32[]{:S(2)}) collective-permute-start(f32[3,1024,1]{1,2,0:T(1,128)S(1)} %get-tuple-element.94), channel_id=1, source_target_pairs={{1,0},{2,1},{3,2},{4,3},{5,4},{6,5},{7,6},{0,7},{9,8},{10,9},{11,1... | collective-permute-start | bytes 36872 | tf_op jit(solution)/shard_map/ppermute | solution.py:22
  70.4 1.4 collective-permute-done
  71.8 3.5 %collective-permute-done.1 = f32[3,1024,1]{1,2,0:T(1,128)S(1)} collective-permute-done((f32[3,1024,1]{1,2,0:T(1,128)S(1)}, f32[3,1024,1]{1,2,0:T(1,128)S(1)}, u32[]{:S(2)}, u32[]{:S(2)}) %collective-permute-start.1) | collective-permute-done | bytes 12320 | tf_op jit(solution)/shard_map/ppermute | solution.py:19
  75.3 2.8 %fusion.34 = (f32[3,1024,64]{1,2,0:T(8,128)S(1)}, f32[3,1024,64]{1,2,0:T(8,128)S(1)}) fusion(f32[3,1024,64]{1,2,0:T(8,128)} %all-reduce.10.cloned.1.call-done, f32[3,1024,1]{1,2,0:T(1,128)S(1)} %collective-permute-done.1, f32[3,1024,1]{1,2,0:T(1,128)S(1)} %collective-permute-done, f32[1024]{0:T(1024)S(1)} %divide_multiply_fusion), kind=kLoop, calls=%fused_computation.57 | loop fusion | flops 1179648 | bytes 2387968 | tf_op jit(solution)/shard_map/mul | solution.py:35
  78.1 1.3 fusion.70
  79.5 0.5 collective-permute-start.3
  80.0 0.5 fusion.18
  80.5 0.2 copy.12
  80.9 3.6 %collective-permute-done.3 = f32[3,1024,1]{1,2,0:T(1,128)S(1)} collective-permute-done((f32[3,1024,1]{1,2,0:T(1,128)S(1)}, f32[3,1024,1]{1,2,0:T(1,128)S(1)}, u32[]{:S(2)}, u32[]{:S(2)}) %collective-permute-start.3) | collective-permute-done | bytes 12320 | tf_op jit(solution)/shard_map/ppermute | solution.py:19
  84.5 0.2 fusion.32
  84.7 0.9 fusion.82
  85.7 0.5 collective-permute-start.5
  86.2 1.3 pad_slice_fusion.7
  87.6 1.1 copy.13
  88.9 1.8 collective-permute-done.5
  90.7 1.1 fusion.57
  91.8 0.2 copy.14
  92.0 0.1 mul.452
  92.2 23.0 %gather_fusion = f32[4096]{0:T(1024)S(1)} fusion(f32[196608]{0:T(1024)S(1)} %pad_maximum_fusion.16, s32[4096]{0:T(1024)S(1)} %get-tuple-element.53), kind=kCustom, calls=%fused_computation | custom fusion | bytes 49152 | tf_op jit(solution)/shard_map/gather | solution.py:70
  115.3 22.2 %scatter_custom_fusion = f32[262144]{0:T(1024)S(1)} fusion(s32[4096]{0:T(1024)S(1)} %compare_select_fusion.1, f32[4096]{0:T(1024)S(1)} %multiply_select_fusion, f32[]{:T(128)} %constant.120.clone.1), kind=kCustom, calls=%fused_computation.71 | custom fusion | flops 4096 | bytes 1048580 | tf_op jit(solution)/shard_map/scatter-add | solution.py:72
  137.5 0.1 slice.347
  137.7 0.2 copy.16
  137.9 1.3 collective-permute-start.6
  139.4 0.1 slice.357
  139.5 0.2 copy.17
  139.7 0.9 collective-permute-done.6
  140.7 3.5 %collective-permute-done.7 = f32[3,1024,1]{1,2,0:T(1,128)S(1)} collective-permute-done((f32[3,1024,1]{1,2,0:T(1,128)S(1)}, f32[3,1024,1]{1,2,0:T(1,128)S(1)}, u32[]{:S(2)}, u32[]{:S(2)}) %collective-permute-start.7) | collective-permute-done | bytes 12320 | tf_op jit(solution)/shard_map/ppermute | solution.py:19
  144.2 0.6 fusion.30
  145.1 0.5 collective-permute-start.9
  145.6 0.2 slice.370
  145.8 0.2 copy.18
  146.0 0.5 collective-permute-done.8
  146.5 3.8 %collective-permute-done.9 = f32[3,1024,1]{1,2,0:T(1,128)S(1)} collective-permute-done((f32[3,1024,1]{1,2,0:T(1,128)S(1)}, f32[3,1024,1]{1,2,0:T(1,128)S(1)}, u32[]{:S(2)}, u32[]{:S(2)}) %collective-permute-start.9) | collective-permute-done | bytes 12320 | tf_op jit(solution)/shard_map/ppermute | solution.py:19
  150.2 0.6 fusion.28
  150.8 0.2 fusion.46
  151.2 0.5 collective-permute-start.11
  151.7 0.9 collective-permute-done.10
  152.6 3.6 %collective-permute-done.11 = f32[3,1024,1]{1,2,0:T(1,128)S(1)} collective-permute-done((f32[3,1024,1]{1,2,0:T(1,128)S(1)}, f32[3,1024,1]{1,2,0:T(1,128)S(1)}, u32[]{:S(2)}, u32[]{:S(2)}) %collective-permute-start.11) | collective-permute-done | bytes 12320 | tf_op jit(solution)/shard_map/ppermute | solution.py:19
  156.2 0.6 fusion.26
  156.8 0.2 fusion.40
  157.0 0.2 fusion.5
  157.3 3.1 %multiply_reduce_fusion = (f32[]{:T(128)}, f32[]{:T(128)}, f32[]{:T(128)}, f32[]{:T(128)}, f32[2,1024,64]{1,2,0:T(8,128)S(1)}) fusion(f32[2,1024,64]{1,2,0:T(8,128)S(1)} %copy-done.3, f32[2,1024,64]{1,2,0:T(8,128)S(1)} %copy-done.1, f32[2,1024,64]{1,2,0:T(8,128)S(1)} %fusion.5, f32[1024,1024]{1,0:T(8,128)S(1)} %copy-done), kind=kOutput, calls=%fused_computation.66 | convolution fusion | flops 1611792384 | bytes 6291472 | tf_op jit(solution)/shard_map/ji,mjc->mic/dot_general | solution.py:79
  160.3 37.2 %all-reduce.7 = (f32[]{:T(128)}, f32[]{:T(128)}, f32[]{:T(128)}, f32[]{:T(128)}) all-reduce(f32[]{:T(128)} %get-tuple-element.41, f32[]{:T(128)} %get-tuple-element.42, f32[]{:T(128)} %get-tuple-element.40, f32[]{:T(128)} %get-tuple-element.39), channel_id=1, replica_groups=mesh['ens'=4,'lon'=8] {'ens','lon'}, use_global_device_ids=true, to_apply=%region_1.0 | all-reduce | flops 4 | bytes 32 | tf_op jit(solution)/shard_map/psum | solution.py:81
  201.5 1.3 multiply_add_fusion
  (52 shorter events, 1.7 us)
Async XLA Ops:
  7.2 6.9 %copy-start.2 = (bf16[2,3,1024,64]{2,3,1,0:T(8,128)(2,1)S(1)}, bf16[2,3,1024,64]{2,3,1,0:T(8,128)(2,1)}, u32[]{:S(2)}) copy-start(bf16[2,3,1024,64]{2,3,1,0:T(8,128)(2,1)} %param.17) | copy-start | bytes 2359300
  7.2 8.1 %copy-start.5 = (s32[4096]{0:T(1024)S(1)}, s32[4096]{0:T(1024)}, u32[]{:S(2)}) copy-start(s32[4096]{0:T(1024)} %param.19) | copy-start | bytes 49156
  7.2 8.1 %copy-start.6 = (s32[4096]{0:T(1024)S(1)}, s32[4096]{0:T(1024)}, u32[]{:S(2)}) copy-start(s32[4096]{0:T(1024)} %param.20) | copy-start | bytes 49156
  7.2 59.5 %all-reduce.10.cloned.1.call-start = ((), (), s32[]{:S(2)}) async-start(), calls=%async_computation | async-start | bytes 1572864 | tf_op jit(solution)/shard_map/psum | solution.py:55
  67.7 4.1 %collective-permute-start = (f32[3,1024,1]{1,2,0:T(1,128)S(1)}, f32[3,1024,1]{1,2,0:T(1,128)S(1)}, u32[]{:S(2)}, u32[]{:S(2)}) collective-permute-start(f32[3,1024,1]{1,2,0:T(1,128)S(1)} %get-tuple-element.94), channel_id=1, source_target_pairs={{1,0},{2,1},{3,2},{4,3},{5,4},{6,5},{7,6},{0,7},{9,8},{10,9},{11,1... | collective-permute-start | bytes 36872 | tf_op jit(solution)/shard_map/ppermute | solution.py:22
  70.4 4.9 %collective-permute-start.1 = (f32[3,1024,1]{1,2,0:T(1,128)S(1)}, f32[3,1024,1]{1,2,0:T(1,128)S(1)}, u32[]{:S(2)}, u32[]{:S(2)}) collective-permute-start(f32[3,1024,1]{1,2,0:T(1,128)S(1)} %get-tuple-element.95), channel_id=1, source_target_pairs={{0,1},{1,2},{2,3},{3,4},{4,5},{5,6},{6,7},{7,0},{8,9},{9,10},{10,1... | collective-permute-start | bytes 36872 | tf_op jit(solution)/shard_map/ppermute | solution.py:19
  79.5 1.5 collective-permute-start.2
  79.5 5.0 %collective-permute-start.3 = (f32[3,1024,1]{1,2,0:T(1,128)S(1)}, f32[3,1024,1]{1,2,0:T(1,128)S(1)}, u32[]{:S(2)}, u32[]{:S(2)}) collective-permute-start(f32[3,1024,1]{1,2,0:T(1,128)S(1)} %get-tuple-element.91), channel_id=1, source_target_pairs={{0,1},{1,2},{2,3},{3,4},{4,5},{5,6},{6,7},{7,0},{8,9},{9,10},{10,1... | collective-permute-start | bytes 36872 | tf_op jit(solution)/shard_map/ppermute | solution.py:19
  85.7 3.2 %collective-permute-start.4 = (f32[3,1024,1]{1,2,0:T(1,128)S(1)}, f32[3,1024,1]{1,2,0:T(1,128)S(1)}, u32[]{:S(2)}, u32[]{:S(2)}) collective-permute-start(f32[3,1024,1]{1,2,0:T(1,128)S(1)} %get-tuple-element.85), channel_id=1, source_target_pairs={{1,0},{2,1},{3,2},{4,3},{5,4},{6,5},{7,6},{0,7},{9,8},{10,9},{11,1... | collective-permute-start | bytes 36872 | tf_op jit(solution)/shard_map/ppermute | solution.py:22
  85.7 5.0 %collective-permute-start.5 = (f32[3,1024,1]{1,2,0:T(1,128)S(1)}, f32[3,1024,1]{1,2,0:T(1,128)S(1)}, u32[]{:S(2)}, u32[]{:S(2)}) collective-permute-start(f32[3,1024,1]{1,2,0:T(1,128)S(1)} %get-tuple-element.84), channel_id=1, source_target_pairs={{0,1},{1,2},{2,3},{3,4},{4,5},{5,6},{6,7},{7,0},{8,9},{9,10},{10,1... | collective-permute-start | bytes 36872 | tf_op jit(solution)/shard_map/ppermute | solution.py:19
  92.2 23.1 %copy-start.7 = (f32[4096]{0:T(1024)S(1)}, f32[4096]{0:T(1024)}, u32[]{:S(2)}) copy-start(f32[4096]{0:T(1024)} %param.21) | copy-start | bytes 49156
  137.9 2.7 %collective-permute-start.6 = (f32[3,1024,1]{1,2,0:T(1,128)S(1)}, f32[3,1024,1]{1,2,0:T(1,128)S(1)}, u32[]{:S(2)}, u32[]{:S(2)}) collective-permute-start(f32[3,1024,1]{1,2,0:T(1,128)S(1)} %get-tuple-element.97), channel_id=1, source_target_pairs={{1,0},{2,1},{3,2},{4,3},{5,4},{6,5},{7,6},{0,7},{9,8},{10,9},{11,1... | collective-permute-start | bytes 36872 | tf_op jit(solution)/shard_map/ppermute | solution.py:22
  139.2 4.9 %collective-permute-start.7 = (f32[3,1024,1]{1,2,0:T(1,128)S(1)}, f32[3,1024,1]{1,2,0:T(1,128)S(1)}, u32[]{:S(2)}, u32[]{:S(2)}) collective-permute-start(f32[3,1024,1]{1,2,0:T(1,128)S(1)} %get-tuple-element.98), channel_id=1, source_target_pairs={{0,1},{1,2},{2,3},{3,4},{4,5},{5,6},{6,7},{7,0},{8,9},{9,10},{10,1... | collective-permute-start | bytes 36872 | tf_op jit(solution)/shard_map/ppermute | solution.py:19
  145.0 1.5 collective-permute-start.8
  145.1 5.2 %collective-permute-start.9 = (f32[3,1024,1]{1,2,0:T(1,128)S(1)}, f32[3,1024,1]{1,2,0:T(1,128)S(1)}, u32[]{:S(2)}, u32[]{:S(2)}) collective-permute-start(f32[3,1024,1]{1,2,0:T(1,128)S(1)} %get-tuple-element.78), channel_id=1, source_target_pairs={{0,1},{1,2},{2,3},{3,4},{4,5},{5,6},{6,7},{7,0},{8,9},{9,10},{10,1... | collective-permute-start | bytes 36872 | tf_op jit(solution)/shard_map/ppermute | solution.py:19
  151.1 1.5 collective-permute-start.10
  151.2 6.0 %copy-start = (f32[1024,1024]{1,0:T(8,128)S(1)}, f32[1024,1024]{1,0:T(8,128)}, u32[]{:S(2)}) copy-start(f32[1024,1024]{1,0:T(8,128)} %param.18) | copy-start | bytes 12582916
  151.2 6.0 %copy-start.1 = (f32[2,1024,64]{1,2,0:T(8,128)S(1)}, f32[2,1024,64]{1,2,0:T(8,128)}, u32[]{:S(2)}) copy-start(f32[2,1024,64]{1,2,0:T(8,128)} %param.16) | copy-start | bytes 1572868
  151.2 6.0 %copy-start.3 = (f32[2,1024,64]{1,2,0:T(8,128)S(1)}, f32[2,1024,64]{1,2,0:T(8,128)}, u32[]{:S(2)}) copy-start(f32[2,1024,64]{1,2,0:T(8,128)} %param.15) | copy-start | bytes 1572868
  151.2 5.0 %collective-permute-start.11 = (f32[3,1024,1]{1,2,0:T(1,128)S(1)}, f32[3,1024,1]{1,2,0:T(1,128)S(1)}, u32[]{:S(2)}, u32[]{:S(2)}) collective-permute-start(f32[3,1024,1]{1,2,0:T(1,128)S(1)} %get-tuple-element.74), channel_id=1, source_target_pairs={{0,1},{1,2},{2,3},{3,4},{4,5},{5,6},{6,7},{7,0},{8,9},{9,10},{10,1... | collective-permute-start | bytes 36872 | tf_op jit(solution)/shard_map/ppermute | solution.py:19
  157.0 44.5 %copy-start.4 = (f32[2,1024,64]{1,2,0:T(8,128)S(1)}, f32[2,1024,64]{1,2,0:T(8,128)}, u32[]{:S(2)}) copy-start(f32[2,1024,64]{1,2,0:T(8,128)} %param.14) | copy-start | bytes 1572868
Sparse Core Ops, SparseCore 0:
  15.3 51.3 all-reduce.9
where the time goes:
time: 211 us; the launch traced here: 210 us
  waiting for transfers between devices  75 us (36%)
  blocking collectives  37.2 us (18%)
  other arithmetic  34.3 us (16%)
  local copies, waits for them, and re-layouts  28.5 us (14%)
  between operations  18.5 us (9%)
  matrix products  9.88 us (5%)
  starting transfers between devices  6.27 us (3%)
    psum x1, waiting for transfers between devices, body(): lat_slab = lax.psum(increment, 'ens')  51.4 us
    psum x1, blocking collectives, body(): lax.psum((jnp.sum(residual * residual), jnp.sum(direction * image_vec), j...  37.2 us
    gather x1, local copies, waits for them, and re-layouts, body(): observed = jnp.concatenate(heights)[gather_index]  23 us
    scatter-add x1, other arithmetic, body(): jnp.zeros(((STEPS + 1) * cells,), jnp.float32).at[slot_index].add(weighted)  22.2 us
    ppermute x6, waiting for transfers between devices, extended(): lax.ppermute(lax.slice_in_dim(block, block.shape[dim] - width, None, axis...  19.8 us
    dot_general x1, matrix products, body(): localized = jnp.einsum('ij,mjc->mic', localize, direction, precision=hi)  6.8 us
    mul x6, other arithmetic, model_step(): 0.5 * metric[:, None] * (lon_wide[:, :, 2:] - lon_wide[:, :, :-2])  4.76 us
    ppermute x6, starting transfers between devices, extended(): lax.ppermute(lax.slice_in_dim(block, 0, width, axis=dim), axis, backward)  4.27 us
  transfers between devices with their start and end apart: 13, of which 12 were waited for; matrix products, arithmetic and copies ran while one was open for 2% of the time, Pallas kernels for 0%

commit v1 on v0

v1 whole, which is shorter than its diff:
```python
import functools

import numpy as np
import jax
import jax.numpy as jnp
from jax import lax
from jax.experimental import pallas as pl
from jax.experimental.pallas import tpu as pltpu
from jax.sharding import PartitionSpec as P

STEPS = 3
HALO = 8
CHUNK = 512
MESH = pl.DeviceIdType.MESH
NT = (((1,), (1,)), ((), ()))
NN = (((1,), (0,)), ((), ()))


def split_bf16(values):
    high = values.astype(jnp.bfloat16)
    low = (values - high.astype(jnp.float32)).astype(jnp.bfloat16)
    return high, low


def dot(left, right, dims):
    return lax.dot_general(left, right, dims, preferred_element_type=jnp.float32)


def grid_constants(lat):
    phi = np.pi * (-1.0 / 3.0 + 2.0 / 3.0 * (np.arange(lat) + 0.5) / lat)
    half = 0.5 * 0.35
    up = np.full(lat, half)
    up[-1] = 0.0
    down = np.full(lat, half)
    down[0] = 0.0
    rows = np.stack([half / np.cos(phi), 0.2 * np.sin(phi), up, down])
    return np.ascontiguousarray(np.broadcast_to(rows[:, None], (4, 8, lat))).astype(np.float32)


def linear_step(source, target, sign, consts, forcing=None):
    rows, lat = source.shape[1], source.shape[2]
    lon_c, cor_c, up_c, down_c = (sign * consts[k] for k in range(4))
    for start in range(0, rows, 8):
        here = pl.ds(start, 8)

        def east(comp, block):
            if start + 8 == rows:
                return pltpu.roll(block, 7, 0)
            return source[comp, pl.ds(start + 1, 8), :]

        def west(comp, block):
            if start == 0:
                return pltpu.roll(block, 1, 0)
            return source[comp, pl.ds(start - 1, 8), :]

        def lat_diff(block):
            return up_c * pltpu.roll(block, lat - 1, 1) - down_c * pltpu.roll(block, 1, 1)

        height, zonal, merid = (source[c, here, :] for c in range(3))
        height_lon = east(0, height) - west(0, height)
        zonal_lon = east(1, zonal) - west(1, zonal)
        target[0, here, :] = height - lon_c * zonal_lon - lat_diff(merid)
        target[1, here, :] = zonal - lon_c * height_lon + cor_c * merid
        target[2, here, :] = merid - lat_diff(height) - cor_c * zonal


def kernel(
    ens, lon, direction, residual, perturb, localize, cell, slot, weight, consts,
    image, scalars,
    high, low, split, stage, arrived, reduced, fields, other, heights, wsum, wmat,
    tiles, tile,
    rs_send, rs_recv, ag_send, ag_recv, halo_send, halo_recv, tile_send, tile_recv,
):
    me_e, me_l = lax.axis_index("ens"), lax.axis_index("lon")
    count = ens * lon
    me = me_e * lon + me_l
    members, cols, lat = direction.shape
    block = lat // ens
    stacked = members * cols

    barrier = pltpu.get_barrier_semaphore()

    def greet(offset, carry):
        peer = lax.rem(me + offset, count)
        pl.semaphore_signal(
            barrier, inc=1, device_id=(peer // lon, lax.rem(peer, lon)), device_id_type=MESH
        )
        return carry

    lax.fori_loop(1, count, greet, 0)

    d_high, d_low = split_bf16(direction[...].reshape(stacked, lat))
    split[pl.ds(0, stacked), :] = d_high
    split[pl.ds(stacked, stacked), :] = d_low

    def localized_block(index, dest):
        at = pl.ds(pl.multiple_of(index * block, block), block)
        l_high, l_low = split_bf16(localize[at, :])
        high[at, :] = l_high
        low[at, :] = l_low
        both = dot(split[...], l_high, NT)
        local = both[:stacked] + both[stacked:] + dot(split[pl.ds(0, stacked), :], l_low, NT)
        for c in range(3):
            total = None
            for m in range(members):
                term = perturb[m, c, :, at].astype(jnp.float32) * local[m * cols:(m + 1) * cols]
                total = term if total is None else total + term
            stage[dest, c] = total

    def peer_of(offset):
        return lax.rem(me_e + offset, ens)

    def first(offset, carry):
        localized_block(peer_of(offset), offset - 1)
        return carry

    def rs_copy(offset, c):
        return pltpu.make_async_remote_copy(
            src_ref=stage.at[offset - 1, c], dst_ref=arrived.at[offset - 1, c],
            send_sem=rs_send.at[offset - 1, c], recv_sem=rs_recv.at[offset - 1, c],
            device_id=(peer_of(offset), me_l), device_id_type=MESH,
        )

    localized_block(peer_of(1), 0)
    pl.semaphore_wait(barrier, count - 1)
    for c in range(3):
        rs_copy(1, c).start()
    for offset in range(2, ens):
        localized_block(peer_of(offset), offset - 1)
        for c in range(3):
            rs_copy(offset, c).start()
    localized_block(me_e, ens - 1)

    wsum[...] = jnp.zeros_like(wsum)
    slots_cols = STEPS * cols

    def weights(step, carry):
        at = pl.ds(pl.multiple_of(step * CHUNK, CHUNK), CHUNK)
        cells, slots, value = cell[:, at], slot[:, at], weight[:, at]
        row = cells // cols
        key = slots * cols + (cells - row * cols)
        v_high, v_low = split_bf16(value)
        v_high, v_low = v_high.astype(jnp.float32), v_low.astype(jnp.float32)
        ids = lax.broadcasted_iota(jnp.int32, (slots_cols, CHUNK), 0)
        hit = ids == key
        left = jnp.concatenate(
            [jnp.where(hit, v_high, 0.0), jnp.where(hit, v_low, 0.0)], axis=0
        ).astype(jnp.bfloat16)
        lat_ids = lax.broadcasted_iota(jnp.int32, (lat, CHUNK), 0)
        right = jnp.where(lat_ids == row, 1.0, 0.0).astype(jnp.bfloat16)
        wsum[...] += dot(left, right, NT)
        return carry

    lax.fori_loop(0, cell.shape[1] // CHUNK, weights, 0)
    for s in range(STEPS):
        wmat[s, pl.ds(HALO, cols), :] = (
            wsum[pl.ds(s * cols, cols), :] + wsum[pl.ds(slots_cols + s * cols, cols), :]
        )

    left_dev = (me_e, lax.rem(me_l + lon - 1, lon))
    right_dev = (me_e, lax.rem(me_l + 1, lon))

    def halo_copies(ref, which):
        west = pltpu.make_async_remote_copy(
            src_ref=ref.at[:, pl.ds(HALO, HALO), :], dst_ref=ref.at[:, pl.ds(HALO + cols, HALO), :],
            send_sem=halo_send.at[which, 0], recv_sem=halo_recv.at[which, 0],
            device_id=left_dev, device_id_type=MESH,
        )
        east = pltpu.make_async_remote_copy(
            src_ref=ref.at[:, pl.ds(cols, HALO), :], dst_ref=ref.at[:, pl.ds(0, HALO), :],
            send_sem=halo_send.at[which, 1], recv_sem=halo_recv.at[which, 1],
            device_id=right_dev, device_id_type=MESH,
        )
        return west, east

    w_copies = halo_copies(wmat, 0)
    for copy in w_copies:
        copy.start()

    mine = pl.ds(pl.multiple_of(me_e * block, block), block)

    def ag_copy(offset, c):
        return pltpu.make_async_remote_copy(
            src_ref=reduced.at[c], dst_ref=fields.at[c, pl.ds(HALO, cols), mine],
            send_sem=ag_send.at[offset - 1, c], recv_sem=ag_recv.at[offset - 1, c],
            device_id=(peer_of(offset), me_l), device_id_type=MESH,
        )

    for c in range(3):
        total = stage[ens - 1, c]
        for offset in range(1, ens):
            rs_copy(offset, c).wait_recv()
            total = total + arrived[offset - 1, c]
        reduced[c] = total
        fields[c, pl.ds(HALO, cols), mine] = total
        for offset in range(1, ens):
            ag_copy(offset, c).start()
    for c in range(3):
        for offset in range(1, ens):
            ag_copy(offset, c).wait_recv()

    f_copies = halo_copies(fields, 1)
    for copy in f_copies:
        copy.start()
    for copy in f_copies:
        copy.wait()

    def forward(source, target, n):
        linear_step(source, target, 1.0, consts)
        heights[n] = target[0]

    forward(fields, other, 0)
    forward(other, fields, 1)
    forward(fields, other, 2)
    for copy in w_copies:
        copy.wait()
    fields[0] = wmat[2] * heights[2]
    fields[1] = jnp.zeros_like(fields[1])
    fields[2] = jnp.zeros_like(fields[2])
    linear_step(fields, other, -1.0, consts)
    other[0] += wmat[1] * heights[1]
    linear_step(other, fields, -1.0, consts)
    fields[0] += wmat[0] * heights[0]
    linear_step(fields, other, -1.0, consts)

    for m in range(members):
        total = None
        for c in range(3):
            term = perturb[m, c].astype(jnp.float32) * other[c, pl.ds(HALO, cols), :]
            total = term if total is None else total + term
        p_high, p_low = split_bf16(total)
        split[pl.ds(m * cols, cols), :] = p_high
        split[pl.ds(stacked + m * cols, cols), :] = p_low

    def pulled(index, sums):
        at = pl.ds(pl.multiple_of(index * block, block), block)
        both = dot(split[...], high[:, at], NN)
        back = both[:stacked] + both[stacked:] + dot(split[pl.ds(0, stacked), :], low[:, at], NN)
        out = []
        d = direction[:, :, at].reshape(stacked, block)
        r = residual[:, :, at].reshape(stacked, block)
        img = d + back
        image[:, :, at] = img.reshape(members, cols, block)
        for total, term in zip(sums, (r * r, d * img, r * img, img * img)):
            term = term.reshape(stacked // 8, 8, block).sum(axis=0)
            for k in range(block // 128):
                total = total + term[:, k * 128:(k + 1) * 128]
            out.append(total)
        return tuple(out)

    sums = lax.fori_loop(0, ens, pulled, tuple(jnp.zeros((8, 128), jnp.float32) for _ in range(4)))
    rows = [jnp.sum(s, axis=0, keepdims=True) for s in sums]
    tile[...] = jnp.concatenate(rows + [jnp.zeros((4, 128), jnp.float32)], axis=0)

    def tell(offset, carry):
        peer = lax.rem(me + offset, count)
        pltpu.make_async_remote_copy(
            src_ref=tile, dst_ref=tiles.at[offset - 1],
            send_sem=tile_send, recv_sem=tile_recv,
            device_id=(peer // lon, lax.rem(peer, lon)), device_id_type=MESH,
        ).start()
        return carry

    lax.fori_loop(1, count, tell, 0)
    for c in range(3):
        for offset in range(1, ens):
            rs_copy(offset, c).wait_send()
            ag_copy(offset, c).wait_send()
    everything = pltpu.make_async_remote_copy(
        src_ref=tiles, dst_ref=tiles, send_sem=tile_send, recv_sem=tile_recv,
        device_id=right_dev, device_id_type=MESH,
    )
    everything.wait_send()
    everything.wait_recv()
    total = jnp.sum(tiles[...], axis=0) + tile[...]
    scalars[...] = jnp.broadcast_to(jnp.sum(total, axis=1, keepdims=True), (8, 128))


def body(ens, lon, control, residual, direction, ens_perturb, localize, obs_cell, obs_slot, obs_weight):
    flip = functools.partial(jnp.swapaxes, axis1=-1, axis2=-2)
    control, residual, direction, ens_perturb = map(flip, (control, residual, direction, ens_perturb))
    members, cols, lat = direction.shape
    nobs = obs_cell.shape[0]
    block = lat // ens
    count = ens * lon
    wide = cols + 2 * HALO
    f32, bf16 = jnp.float32, jnp.bfloat16
    vmem = pl.BlockSpec(memory_space=pltpu.VMEM)
    dma = pltpu.SemaphoreType.DMA
    image, scalars = pl.pallas_call(
        functools.partial(kernel, ens, lon),
        out_shape=(
            jax.ShapeDtypeStruct((members, cols, lat), f32),
            jax.ShapeDtypeStruct((8, 128), f32),
        ),
        in_specs=[vmem] * 8,
        out_specs=(vmem, vmem),
        scratch_shapes=[
            pltpu.VMEM((lat, lat), bf16),
            pltpu.VMEM((lat, lat), bf16),
            pltpu.VMEM((2 * members * cols, lat), bf16),
            pltpu.VMEM((ens, 3, cols, block), f32),
            pltpu.VMEM((ens - 1, 3, cols, block), f32),
            pltpu.VMEM((3, cols, block), f32),
            pltpu.VMEM((3, wide, lat), f32),
            pltpu.VMEM((3, wide, lat), f32),
            pltpu.VMEM((STEPS, wide, lat), f32),
            pltpu.VMEM((2 * STEPS * cols, lat), f32),
            pltpu.VMEM((STEPS, wide, lat), f32),
            pltpu.VMEM((count - 1, 8, 128), f32),
            pltpu.VMEM((8, 128), f32),
            dma((ens - 1, 3)), dma((ens - 1, 3)),
            dma((ens - 1, 3)), dma((ens - 1, 3)),
            dma((2, 2)), dma((2, 2)),
            dma, dma,
        ],
        compiler_params=pltpu.CompilerParams(collective_id=0, has_side_effects=True),
    )(
        direction, residual, ens_perturb, localize,
        obs_cell.reshape(1, nobs), obs_slot.reshape(1, nobs), obs_weight.reshape(1, nobs),
        jnp.asarray(grid_constants(lat)),
    )
    norm_old, curvature, cross_term, square = (scalars[k, 0] for k in range(4))
    step_size = norm_old / curvature
    control_new = control + step_size * direction
    residual_new = residual - step_size * image
    norm_new = norm_old - 2.0 * step_size * cross_term + step_size * step_size * square
    direction_new = residual_new + norm_new / norm_old * direction
    return tuple(map(flip, (control_new, residual_new, direction_new)))


def solution(mesh):
    fields = P("ens", None, "lon")
    in_specs = (fields, fields, fields, P("ens", None, None, "lon"), P(), P("lon"), P("lon"), P("lon"))
    ens, lon = mesh.shape["ens"], mesh.shape["lon"]
    return jax.shard_map(
        functools.partial(body, ens, lon), mesh=mesh, in_specs=in_specs,
        out_specs=(fields, fields, fields), check_vma=False,
    )
```

time: 211 us -> 51.9 us (0.25)
  waiting for transfers between devices: 75 us -> 0 us
  Pallas kernels: 0 us -> 42.9 us
  blocking collectives: 37.2 us -> 0 us
  other arithmetic: 34.3 us -> 2.98 us
  local copies, waits for them, and re-layouts: 28.5 us -> 1.36 us
  between operations: 18.5 us -> 4.41 us
  matrix products: 9.88 us -> 0 us
  starting transfers between devices: 6.27 us -> 0 us
    psum x1 -> x0, waiting for transfers between devices: 51.4 us -> none  [body(): lat_slab = lax.psum(increment, 'ens')]
    pallas_call x0 -> x1, Pallas kernels: none -> 42.9 us  [body(): pl.pallas_call(functools.partial(kernel, ens, lon), out_shape=(jax.ShapeD...]
    psum x1 -> x0, blocking collectives: 37.2 us -> none  [body(): lax.psum((jnp.sum(residual * residual), jnp.sum(direction * image_vec), j...]
    ppermute x12 -> x0, waiting for transfers between devices: 23.6 us -> none  [the longest x6 19.8 us: extended(): lax.ppermute(lax.slice_in_dim(block, block.shape[dim] - width, None, axis...]
    gather x1 -> x0, local copies, waits for them, and re-layouts: 23 us -> none  [body(): observed = jnp.concatenate(heights)[gather_index]]
    scatter-add x3 -> x0, other arithmetic: 22.3 us -> none  [the longest x1 22.2 us: body(): jnp.zeros(((STEPS + 1) * cells,), jnp.float32).at[slot_index].add(weighted)]
    dot_general x2 -> x0, matrix products: 9.88 us -> none  [the longest x1 6.8 us: body(): localized = jnp.einsum('ij,mjc->mic', localize, direction, precision=hi)]
    mul x11 -> x0, other arithmetic: 6.43 us -> none  [the longest x6 4.76 us: model_step(): 0.5 * metric[:, None] * (lon_wide[:, :, 2:] - lon_wide[:, :, :-2])]
  transfers between devices with their start and end apart: 13 -> 0, of which waited for: 12 -> 0; matrix products, arithmetic and copies ran while one was open for 2% -> 0% of each run, Pallas kernels for 0% -> 0%
where the time goes in v1:
time: 51.9 us; the launch traced here: 51.7 us
  Pallas kernels  42.9 us (83%)
  between operations  4.41 us (8%)
  other arithmetic  2.98 us (6%)
  local copies, waits for them, and re-layouts  1.36 us (3%)
    pallas_call x1, Pallas kernels, body(): pl.pallas_call(functools.partial(kernel, ens, lon), out_shape=(jax.ShapeD...  42.9 us
    transpose x1, other arithmetic, body(): return tuple(map(flip, (control_new, residual_new, direction_new)))  2.13 us
    slice x1, local copies, waits for them, and re-layouts, body(): norm_old, curvature, cross_term, square = (scalars[k, 0] for k in range(4))  1.34 us

profile of v1, /device:TPU:0, one launch (start us, length us, event | category | flops | bytes accessed | tf_op | source)
XLA Modules:
  0.0 51.7 jit_solution(12662024720918053914)
XLA Ops:
  0.6 0.0 copy-start
  0.6 0.0 copy-start.1
  0.7 0.0 copy-start.2
  0.7 42.9 %shard_map.112 = (f32[2,64,1024]{2,1,0:T(8,128)}, f32[8,128]{1,0:T(8,128)}) custom-call(f32[2,64,1024]{2,1,0:T(8,128)} %bitcast.17, f32[2,64,1024]{2,1,0:T(8,128)} %bitcast.18, bf16[2,3,64,1024]{3,2,1,0:T(8,128)(2,1)} %bitcast.19, f32[1024,1024]{1,0:T(8,128)} %localize.1, s32[1,4096]{1,0:T(1,128)} %bitcast.20, s32[1,4096]{1,0:T(1,128)} %bitcast.21, ...), custom_call_target="tpu_custom_call" | custom-call | tf_op jit(solution)/shard_map/pallas_call | solution.py:290
  43.6 1.3 %fusion.1 = (f32[1,1]{1,0:T(1,128)}, f32[1,1]{1,0:T(1,128)}, f32[1,1]{1,0:T(1,128)}, f32[1,1]{1,0:T(1,128)}) fusion(f32[8,128]{1,0:T(8,128)} %get-tuple-element.5), kind=kLoop, calls=%fused_computation.4 | loop fusion | bytes 32 | tf_op jit(solution)/shard_map/slice | solution.py:323
  48.6 0.0 copy-done
  48.7 0.0 copy-done.1
  48.7 2.1 %add_bitcast_fusion = (f32[2,1024,64]{1,2,0:T(8,128)}, f32[2,1024,64]{1,2,0:T(8,128)}) fusion(f32[]{:T(128)S(6)} %div.7, f32[2,64,1024]{2,1,0:T(8,128)} %get-tuple-element.6, f32[]{:T(128)S(6)} %div.6, f32[2,1024,64]{1,2,0:T(8,128)S(1)} %copy-done.1, f32[2,1024,64]{1,2,0:T(8,128)S(1)} %copy-done), kind=kLoop, calls=%fused_computation | loop fusion | flops 524288 | bytes 2621448 | tf_op jit(solution)/shard_map/transpose | solution.py:329
  50.8 0.0 copy-done.2
  50.8 0.9 %multiply_add_fusion = f32[2,1024,64]{1,2,0:T(8,128)} fusion(f32[2,1024,64]{1,2,0:T(8,128)S(1)} %copy-done.2, f32[2,1024,64]{1,2,0:T(8,128)S(1)} %copy-done, f32[]{:T(128)S(6)} %div.6), kind=kLoop, calls=%fused_computation.2 | loop fusion | flops 262144 | bytes 1572868 | tf_op jit(solution)/shard_map/add | solution.py:325
Async XLA Ops:
  0.6 48.0 %copy-start = (f32[2,1024,64]{1,2,0:T(8,128)S(1)}, f32[2,1024,64]{1,2,0:T(8,128)}, u32[]{:S(2)}) copy-start(f32[2,1024,64]{1,2,0:T(8,128)} %param.11) | copy-start | bytes 1572868
  0.6 48.0 %copy-start.1 = (f32[2,1024,64]{1,2,0:T(8,128)S(1)}, f32[2,1024,64]{1,2,0:T(8,128)}, u32[]{:S(2)}) copy-start(f32[2,1024,64]{1,2,0:T(8,128)} %param.10) | copy-start | bytes 1572868
  0.7 50.1 %copy-start.2 = (f32[2,1024,64]{1,2,0:T(8,128)S(1)}, f32[2,1024,64]{1,2,0:T(8,128)}, u32[]{:S(2)}) copy-start(f32[2,1024,64]{1,2,0:T(8,128)} %param.9) | copy-start | bytes 1572868

commit v2 on v1

--- a/solution.py
+++ b/solution.py
@@ -1,4 +1,5 @@
 import functools
+import itertools
 
 import numpy as np
 import jax
@@ -64,19 +65,56 @@
         target[2, here, :] = merid - lat_diff(height) - cor_c * zonal
 
 
+def factors(ens):
+    first = 2 if ens % 2 == 0 else 1
+    return first, ens // first
+
+
+def copy_count(ens):
+    na, nb = factors(ens)
+    cross = (na - 1) * (nb - 1)
+    return 3 * (4 * cross + 3 * (na - 1 + nb - 1)) + 8
+
+
 def kernel(
-    ens, lon, direction, residual, perturb, localize, cell, slot, weight, consts,
-    image, scalars,
-    high, low, split, stage, arrived, reduced, fields, other, heights, wsum, wmat,
-    tiles, tile,
-    rs_send, rs_recv, ag_send, ag_recv, halo_send, halo_recv, tile_send, tile_recv,
+    ens, lon, direction, residual_hbm, perturb_hbm, localize_hbm, cell, slot, weight, consts,
+    image, step_row, ratio_row,
+    localize, residual, perturb, high, low, split, stage, relay0, relay1, arr_a, arr_b,
+    reduced, fields, other, heights, wsum, wmat, tiles, tile,
+    load_sem, send_sem, recv_sem, tile_send, tile_recv,
 ):
+    na, nb = factors(ens)
     me_e, me_l = lax.axis_index("ens"), lax.axis_index("lon")
+    me_a, me_b = me_e // nb, lax.rem(me_e, nb)
     count = ens * lon
     me = me_e * lon + me_l
     members, cols, lat = direction.shape
     block = lat // ens
+    half = cols // 2
     stacked = members * cols
+    halves = (pl.ds(0, half), pl.ds(half, half))
+    inner = (pl.ds(HALO, half), pl.ds(HALO + half, half))
+
+    def ens_of(i, j):
+        return lax.rem(me_a + i, na) * nb + lax.rem(me_b + j, nb)
+
+    def lanes_of(index):
+        return pl.ds(pl.multiple_of(index * block, block), block)
+
+    order = [(i, j) for i in range(1, na) for j in range(1, nb)]
+    order += [(0, j) for j in range(1, nb)] + [(i, 0) for i in range(1, na)] + [(0, 0)]
+
+    loads = {}
+    for k, (i, j) in enumerate(order):
+        at = lanes_of(ens_of(i, j))
+        loads[i, j] = pltpu.make_async_copy(localize_hbm.at[at, :], localize.at[at, :], load_sem.at[k])
+    load_p = pltpu.make_async_copy(perturb_hbm, perturb, load_sem.at[ens])
+    load_r = pltpu.make_async_copy(residual_hbm, residual, load_sem.at[ens + 1])
+    loads[order[0]].start()
+    load_p.start()
+    for key in order[1:]:
+        loads[key].start()
+    load_r.start()
 
     barrier = pltpu.get_barrier_semaphore()
 
@@ -89,47 +127,69 @@
 
     lax.fori_loop(1, count, greet, 0)
 
+    ids = itertools.count()
+
+    def remote(src, dst, device):
+        k = next(ids)
+        return pltpu.make_async_remote_copy(
+            src_ref=src, dst_ref=dst, send_sem=send_sem.at[k], recv_sem=recv_sem.at[k],
+            device_id=device, device_id_type=MESH,
+        )
+
     d_high, d_low = split_bf16(direction[...].reshape(stacked, lat))
     split[pl.ds(0, stacked), :] = d_high
     split[pl.ds(stacked, stacked), :] = d_low
 
-    def localized_block(index, dest):
-        at = pl.ds(pl.multiple_of(index * block, block), block)
+    def localized_block(i, j):
+        index = ens_of(i, j)
+        at = lanes_of(index)
+        loads[i, j].wait()
         l_high, l_low = split_bf16(localize[at, :])
         high[at, :] = l_high
         low[at, :] = l_low
         both = dot(split[...], l_high, NT)
         local = both[:stacked] + both[stacked:] + dot(split[pl.ds(0, stacked), :], l_low, NT)
+        if (i, j) == order[0]:
+            load_p.wait()
         for c in range(3):
             total = None
             for m in range(members):
                 term = perturb[m, c, :, at].astype(jnp.float32) * local[m * cols:(m + 1) * cols]
                 total = term if total is None else total + term
-            stage[dest, c] = total
-
-    def peer_of(offset):
-        return lax.rem(me_e + offset, ens)
-
-    def first(offset, carry):
-        localized_block(peer_of(offset), offset - 1)
-        return carry
-
-    def rs_copy(offset, c):
-        return pltpu.make_async_remote_copy(
-            src_ref=stage.at[offset - 1, c], dst_ref=arrived.at[offset - 1, c],
-            send_sem=rs_send.at[offset - 1, c], recv_sem=rs_recv.at[offset - 1, c],
-            device_id=(peer_of(offset), me_l), device_id_type=MESH,
-        )
-
-    localized_block(peer_of(1), 0)
-    pl.semaphore_wait(barrier, count - 1)
-    for c in range(3):
-        rs_copy(1, c).start()
-    for offset in range(2, ens):
-        localized_block(peer_of(offset), offset - 1)
+            stage[i * nb + j, c] = total
+
+    def a_peer(i):
+        return (ens_of(i, 0), me_l)
+
+    def b_peer(j):
+        return (ens_of(0, j), me_l)
+
+    def part(i, j, c, h):
+        return stage.at[i * nb + j, c, halves[h]]
+
+    sum0, sum1, direct, relayed0, relayed1 = {}, {}, {}, {}, {}
+    for c in range(3):
+        for i in range(1, na):
+            for j in range(1, nb):
+                sum0[i, j, c] = remote(part(i, j, c, 0), relay0.at[j - 1, i - 1, c], b_peer(j))
+                sum1[i, j, c] = remote(part(i, j, c, 1), relay1.at[i - 1, j - 1, c], a_peer(i))
+        for j in range(1, nb):
+            direct[0, j, c] = remote(part(0, j, c, 0), arr_b.at[j - 1, c, halves[0]], b_peer(j))
+            relayed1[j, c] = remote(part(0, j, c, 1), arr_b.at[j - 1, c, halves[1]], b_peer(j))
+        for i in range(1, na):
+            direct[i, 0, c] = remote(part(i, 0, c, 1), arr_a.at[i - 1, c, halves[1]], a_peer(i))
+            relayed0[i, c] = remote(part(i, 0, c, 0), arr_a.at[i - 1, c, halves[0]], a_peer(i))
+
+    for k, (i, j) in enumerate(order):
+        localized_block(i, j)
+        if k == 0:
+            pl.semaphore_wait(barrier, count - 1)
         for c in range(3):
-            rs_copy(offset, c).start()
-    localized_block(me_e, ens - 1)
+            if i and j:
+                sum0[i, j, c].start()
+                sum1[i, j, c].start()
+            elif i or j:
+                direct[i, j, c].start()
 
     wsum[...] = jnp.zeros_like(wsum)
     slots_cols = STEPS * cols
@@ -151,7 +211,23 @@
         wsum[...] += dot(left, right, NT)
         return carry
 
-    lax.fori_loop(0, cell.shape[1] // CHUNK, weights, 0)
+    chunks = cell.shape[1] // CHUNK
+    early = chunks // 2
+    lax.fori_loop(0, early, weights, 0)
+
+    for c in range(3):
+        for i in range(1, na):
+            for j in range(1, nb):
+                sum0[i, j, c].wait_recv()
+                stage[i * nb, c, halves[0]] += relay0[j - 1, i - 1, c]
+            relayed0[i, c].start()
+        for j in range(1, nb):
+            for i in range(1, na):
+                sum1[i, j, c].wait_recv()
+                stage[j, c, halves[1]] += relay1[i - 1, j - 1, c]
+            relayed1[j, c].start()
+
+    lax.fori_loop(early, chunks, weights, 0)
     for s in range(STEPS):
         wmat[s, pl.ds(HALO, cols), :] = (
             wsum[pl.ds(s * cols, cols), :] + wsum[pl.ds(slots_cols + s * cols, cols), :]
@@ -161,47 +237,71 @@
     right_dev = (me_e, lax.rem(me_l + 1, lon))
 
     def halo_copies(ref, which):
-        west = pltpu.make_async_remote_copy(
-            src_ref=ref.at[:, pl.ds(HALO, HALO), :], dst_ref=ref.at[:, pl.ds(HALO + cols, HALO), :],
-            send_sem=halo_send.at[which, 0], recv_sem=halo_recv.at[which, 0],
-            device_id=left_dev, device_id_type=MESH,
+        return (
+            remote(ref.at[which, pl.ds(HALO, HALO), :], ref.at[which, pl.ds(HALO + cols, HALO), :], left_dev),
+            remote(ref.at[which, pl.ds(cols, HALO), :], ref.at[which, pl.ds(0, HALO), :], right_dev),
         )
-        east = pltpu.make_async_remote_copy(
-            src_ref=ref.at[:, pl.ds(cols, HALO), :], dst_ref=ref.at[:, pl.ds(0, HALO), :],
-            send_sem=halo_send.at[which, 1], recv_sem=halo_recv.at[which, 1],
-            device_id=right_dev, device_id_type=MESH,
-        )
-        return west, east
-
-    w_copies = halo_copies(wmat, 0)
+
+    w_copies = (
+        remote(wmat.at[:, pl.ds(HALO, HALO), :], wmat.at[:, pl.ds(HALO + cols, HALO), :], left_dev),
+        remote(wmat.at[:, pl.ds(cols, HALO), :], wmat.at[:, pl.ds(0, HALO), :], right_dev),
+    )
     for copy in w_copies:
         copy.start()
 
-    mine = pl.ds(pl.multiple_of(me_e * block, block), block)
-
-    def ag_copy(offset, c):
-        return pltpu.make_async_remote_copy(
-            src_ref=reduced.at[c], dst_ref=fields.at[c, pl.ds(HALO, cols), mine],
-            send_sem=ag_send.at[offset - 1, c], recv_sem=ag_recv.at[offset - 1, c],
-            device_id=(peer_of(offset), me_l), device_id_type=MESH,
-        )
-
-    for c in range(3):
-        total = stage[ens - 1, c]
-        for offset in range(1, ens):
-            rs_copy(offset, c).wait_recv()
-            total = total + arrived[offset - 1, c]
+    mine = lanes_of(me_e)
+    own_a, own_b, pass_a, pass_b = {}, {}, {}, {}
+    for c in range(3):
+        whole = fields.at[c, pl.ds(HALO, cols), mine]
+        for i in range(1, na):
+            own_a[i, c] = remote(reduced.at[c], whole, a_peer(i))
+        for j in range(1, nb):
+            own_b[j, c] = remote(reduced.at[c], whole, b_peer(j))
+        for i in range(1, na):
+            for j in range(1, nb):
+                from_b = lanes_of(me_a * nb + lax.rem(me_b + nb - j, nb))
+                from_a = lanes_of(lax.rem(me_a + na - i, na) * nb + me_b)
+                spot0 = fields.at[c, inner[0], from_b]
+                spot1 = fields.at[c, inner[1], from_a]
+                pass_a[i, j, c] = remote(spot0, spot0, a_peer(i))
+                pass_b[i, j, c] = remote(spot1, spot1, b_peer(j))
+
+    for c in range(3):
+        total = stage[0, c]
+        for j in range(1, nb):
+            direct[0, j, c].wait_recv()
+            relayed1[j, c].wait_recv()
+            total = total + arr_b[j - 1, c]
+        for i in range(1, na):
+            direct[i, 0, c].wait_recv()
+            relayed0[i, c].wait_recv()
+            total = total + arr_a[i - 1, c]
         reduced[c] = total
         fields[c, pl.ds(HALO, cols), mine] = total
-        for offset in range(1, ens):
-            ag_copy(offset, c).start()
-    for c in range(3):
-        for offset in range(1, ens):
-            ag_copy(offset, c).wait_recv()
-
-    f_copies = halo_copies(fields, 1)
-    for copy in f_copies:
-        copy.start()
+        for copy in [own_a[i, c] for i in range(1, na)] + [own_b[j, c] for j in range(1, nb)]:
+            copy.start()
+    load_r.wait()
+    for c in range(3):
+        for j in range(1, nb):
+            own_b[j, c].wait_recv()
+            for i in range(1, na):
+                pass_a[i, j, c].start()
+        for i in range(1, na):
+            own_a[i, c].wait_recv()
+            for j in range(1, nb):
+                pass_b[i, j, c].start()
+    f_copies = []
+    for c in range(3):
+        for i in range(1, na):
+            for j in range(1, nb):
+                pass_a[i, j, c].wait_recv()
+                pass_b[i, j, c].wait_recv()
+        for copy in halo_copies(fields, c):
+            copy.start()
+            f_copies.append(copy)
+    for group in (pass_a, pass_b):
+        for copy in group.values():
+            copy.wait_send()
     for copy in f_copies:
         copy.wait()
 
@@ -233,7 +333,7 @@
         split[pl.ds(stacked + m * cols, cols), :] = p_low
 
     def pulled(index, sums):
-        at = pl.ds(pl.multiple_of(index * block, block), block)
+        at = lanes_of(index)
         both = dot(split[...], high[:, at], NN)
         back = both[:stacked] + both[stacked:] + dot(split[pl.ds(0, stacked), :], low[:, at], NN)
         out = []
@@ -250,7 +350,13 @@
 
     sums = lax.fori_loop(0, ens, pulled, tuple(jnp.zeros((8, 128), jnp.float32) for _ in range(4)))
     rows = [jnp.sum(s, axis=0, keepdims=True) for s in sums]
-    tile[...] = jnp.concatenate(rows + [jnp.zeros((4, 128), jnp.float32)], axis=0)
+    lane = lax.broadcasted_iota(jnp.int32, (1, 128), 1) // 32
+    packed = jnp.zeros((1, 128), jnp.float32)
+    for k, row in enumerate(rows):
+        row = row + pltpu.roll(row, 64, 1)
+        row = row + pltpu.roll(row, 32, 1)
+        packed = jnp.where(lane == k, row, packed)
+    tile[...] = packed
 
     def tell(offset, carry):
         peer = lax.rem(me + offset, count)
@@ -262,10 +368,9 @@
         return carry
 
     lax.fori_loop(1, count, tell, 0)
-    for c in range(3):
-        for offset in range(1, ens):
-            rs_copy(offset, c).wait_send()
-            ag_copy(offset, c).wait_send()
+    for group in (sum0, sum1, direct, relayed0, relayed1, own_a, own_b):
+        for copy in group.values():
+            copy.wait_send()
     everything = pltpu.make_async_remote_copy(
         src_ref=tiles, dst_ref=tiles, send_sem=tile_send, recv_sem=tile_recv,
         device_id=right_dev, device_id_type=MESH,
@@ -273,7 +378,13 @@
     everything.wait_send()
     everything.wait_recv()
     total = jnp.sum(tiles[...], axis=0) + tile[...]
-    scalars[...] = jnp.broadcast_to(jnp.sum(total, axis=1, keepdims=True), (8, 128))
+    norm_old, curvature, cross_term, square = (
+        jnp.sum(jnp.where(lane == k, total, 0.0), axis=1, keepdims=True) for k in range(4)
+    )
+    step_size = norm_old / curvature
+    norm_new = norm_old - 2.0 * step_size * cross_term + step_size * step_size * square
+    step_row[...] = jnp.broadcast_to(step_size, step_row.shape)
+    ratio_row[...] = jnp.broadcast_to(norm_new / norm_old, ratio_row.shape)
 
 
 def body(ens, lon, control, residual, direction, ens_perturb, localize, obs_cell, obs_slot, obs_weight):
@@ -282,36 +393,41 @@
     members, cols, lat = direction.shape
     nobs = obs_cell.shape[0]
     block = lat // ens
+    na, nb = factors(ens)
+    pa, pb = max(na - 1, 1), max(nb - 1, 1)
     count = ens * lon
     wide = cols + 2 * HALO
     f32, bf16 = jnp.float32, jnp.bfloat16
     vmem = pl.BlockSpec(memory_space=pltpu.VMEM)
+    outside = pl.BlockSpec(memory_space=pl.ANY)
     dma = pltpu.SemaphoreType.DMA
-    image, scalars = pl.pallas_call(
+    row = jax.ShapeDtypeStruct((1, lat), f32)
+    image, step_size, ratio = pl.pallas_call(
         functools.partial(kernel, ens, lon),
-        out_shape=(
-            jax.ShapeDtypeStruct((members, cols, lat), f32),
-            jax.ShapeDtypeStruct((8, 128), f32),
-        ),
-        in_specs=[vmem] * 8,
-        out_specs=(vmem, vmem),
+        out_shape=(jax.ShapeDtypeStruct((members, cols, lat), f32), row, row),
+        in_specs=[vmem, outside, outside, outside] + [vmem] * 4,
+        out_specs=(vmem, vmem, vmem),
         scratch_shapes=[
+            pltpu.VMEM((lat, lat), f32),
+            pltpu.VMEM((members, cols, lat), f32),
+            pltpu.VMEM((members, 3, cols, lat), bf16),
             pltpu.VMEM((lat, lat), bf16),
             pltpu.VMEM((lat, lat), bf16),
             pltpu.VMEM((2 * members * cols, lat), bf16),
             pltpu.VMEM((ens, 3, cols, block), f32),
-            pltpu.VMEM((ens - 1, 3, cols, block), f32),
+            pltpu.VMEM((pb, pa, 3, cols // 2, block), f32),
+            pltpu.VMEM((pa, pb, 3, cols // 2, block), f32),
+            pltpu.VMEM((pa, 3, cols, block), f32),
+            pltpu.VMEM((pb, 3, cols, block), f32),
             pltpu.VMEM((3, cols, block), f32),
             pltpu.VMEM((3, wide, lat), f32),
             pltpu.VMEM((3, wide, lat), f32),
             pltpu.VMEM((STEPS, wide, lat), f32),
             pltpu.VMEM((2 * STEPS * cols, lat), f32),
             pltpu.VMEM((STEPS, wide, lat), f32),
-            pltpu.VMEM((count - 1, 8, 128), f32),
-            pltpu.VMEM((8, 128), f32),
-            dma((ens - 1, 3)), dma((ens - 1, 3)),
-            dma((ens - 1, 3)), dma((ens - 1, 3)),
-            dma((2, 2)), dma((2, 2)),
+            pltpu.VMEM((count - 1, 1, 128), f32),
+            pltpu.VMEM((1, 128), f32),
+            dma((ens + 2,)), dma((copy_count(ens),)), dma((copy_count(ens),)),
             dma, dma,
         ],
         compiler_params=pltpu.CompilerParams(collective_id=0, has_side_effects=True),
@@ -320,12 +436,9 @@
         obs_cell.reshape(1, nobs), obs_slot.reshape(1, nobs), obs_weight.reshape(1, nobs),
         jnp.asarray(grid_constants(lat)),
     )
-    norm_old, curvature, cross_term, square = (scalars[k, 0] for k in range(4))
-    step_size = norm_old / curvature
     control_new = control + step_size * direction
     residual_new = residual - step_size * image
-    norm_new = norm_old - 2.0 * step_size * cross_term + step_size * step_size * square
-    direction_new = residual_new + norm_new / norm_old * direction
+    direction_new = residual_new + ratio * direction
     return tuple(map(flip, (control_new, residual_new, direction_new)))
 
 

time: 51.9 us -> 43.8 us (0.84)
  between operations: 4.41 us -> 0.68 us
  Pallas kernels: 42.9 us -> 39.2 us
  local copies, waits for them, and re-layouts: 1.36 us -> 0.01 us
  other arithmetic: 2.98 us -> 3.7 us
    pallas_call x1, Pallas kernels: 42.9 us -> 39.2 us  [body(): pl.pallas_call(functools.partial(kernel, ens, lon), out_shape=(jax.ShapeD...]
    slice x1 -> x0, local copies, waits for them, and re-layouts: 1.34 us -> none  [body(): norm_old, curvature, cross_term, square = (scalars[k, 0] for k in range(4))]
    add x1, other arithmetic: 0.85 us -> 1.54 us  [body(): control_new = control + step_size * direction]
where the time goes in v2:
time: 43.8 us; the launch traced here: 43.6 us
  Pallas kernels  39.2 us (89%)
  other arithmetic  3.7 us (8%)
  between operations  0.68 us (2%)
    pallas_call x1, Pallas kernels, body(): pl.pallas_call(functools.partial(kernel, ens, lon), out_shape=(jax.ShapeD...  39.2 us
    transpose x1, other arithmetic, body(): return tuple(map(flip, (control_new, residual_new, direction_new)))  2.17 us
    add x1, other arithmetic, body(): control_new = control + step_size * direction  1.54 us

profile of v2, /device:TPU:0, one launch (start us, length us, event | category | flops | bytes accessed | tf_op | source)
XLA Modules:
  0.0 43.6 jit_solution(736577735012363417)
XLA Ops:
  0.6 0.0 copy-start
  0.6 0.0 copy-start.1
  0.7 0.0 copy-start.2
  0.7 39.2 %shard_map.112 = (f32[2,64,1024]{2,1,0:T(8,128)}, f32[1,1024]{1,0:T(1,128)}, f32[1,1024]{1,0:T(1,128)}) custom-call(f32[2,64,1024]{2,1,0:T(8,128)} %bitcast.15, f32[2,64,1024]{2,1,0:T(8,128)} %bitcast.16, bf16[2,3,64,1024]{3,2,1,0:T(8,128)(2,1)} %bitcast.17, f32[1024,1024]{1,0:T(8,128)} %localize_hbm.1, s32[1,4096]{1,0:T(1,128)} %bitcast.18, ...), custom_call_target="tpu_custom_call" | custom-call | tf_op jit(solution)/shard_map/pallas_call | solution.py:405
  39.8 0.0 copy-done
  39.9 0.0 copy-done.1
  39.9 2.2 %add_bitcast_fusion = (f32[2,1024,64]{1,2,0:T(8,128)}, f32[2,1024,64]{1,2,0:T(8,128)}) fusion(f32[1024]{0:T(1024)} %bitcast.23, f32[2,64,1024]{2,1,0:T(8,128)} %get-tuple-element.7, f32[1024]{0:T(1024)} %bitcast.21, f32[2,1024,64]{1,2,0:T(8,128)S(1)} %copy-done.1, f32[2,1024,64]{1,2,0:T(8,128)S(1)} %copy-done), kind=kLoop, calls=%fused_computation | loop fusion | flops 524288 | bytes 2629632 | tf_op jit(solution)/shard_map/transpose | solution.py:442
  42.0 0.0 copy-done.2
  42.0 1.5 %multiply_add_fusion = f32[2,1024,64]{1,2,0:T(8,128)} fusion(f32[2,1024,64]{1,2,0:T(8,128)S(1)} %copy-done.2, f32[2,1024,64]{1,2,0:T(8,128)S(1)} %copy-done, f32[1024]{0:T(1024)} %bitcast.22), kind=kLoop, calls=%fused_computation.2 | loop fusion | flops 262144 | bytes 1576960 | tf_op jit(solution)/shard_map/add | solution.py:439
Async XLA Ops:
  0.6 39.2 %copy-start = (f32[2,1024,64]{1,2,0:T(8,128)S(1)}, f32[2,1024,64]{1,2,0:T(8,128)}, u32[]{:S(2)}) copy-start(f32[2,1024,64]{1,2,0:T(8,128)} %param.11) | copy-start | bytes 1572868
  0.6 39.2 %copy-start.1 = (f32[2,1024,64]{1,2,0:T(8,128)S(1)}, f32[2,1024,64]{1,2,0:T(8,128)}, u32[]{:S(2)}) copy-start(f32[2,1024,64]{1,2,0:T(8,128)} %param.10) | copy-start | bytes 1572868
  0.7 41.4 %copy-start.2 = (f32[2,1024,64]{1,2,0:T(8,128)S(1)}, f32[2,1024,64]{1,2,0:T(8,128)}, u32[]{:S(2)}) copy-start(f32[2,1024,64]{1,2,0:T(8,128)} %param.9) | copy-start | bytes 1572868

commit v3 on v2

--- a/solution.py
+++ b/solution.py
@@ -38,10 +38,10 @@
     return np.ascontiguousarray(np.broadcast_to(rows[:, None], (4, 8, lat))).astype(np.float32)
 
 
-def linear_step(source, target, sign, consts, forcing=None):
+def linear_step(source, target, sign, consts, blocks):
     rows, lat = source.shape[1], source.shape[2]
     lon_c, cor_c, up_c, down_c = (sign * consts[k] for k in range(4))
-    for start in range(0, rows, 8):
+    for start in blocks:
         here = pl.ds(start, 8)
 
         def east(comp, block):
@@ -212,7 +212,7 @@
         return carry
 
     chunks = cell.shape[1] // CHUNK
-    early = chunks // 2
+    early, late = chunks * 3 // 8, chunks * 5 // 8
     lax.fori_loop(0, early, weights, 0)
 
     for c in range(3):
@@ -227,11 +227,7 @@
                 stage[j, c, halves[1]] += relay1[i - 1, j - 1, c]
             relayed1[j, c].start()
 
-    lax.fori_loop(early, chunks, weights, 0)
-    for s in range(STEPS):
-        wmat[s, pl.ds(HALO, cols), :] = (
-            wsum[pl.ds(s * cols, cols), :] + wsum[pl.ds(slots_cols + s * cols, cols), :]
-        )
+    lax.fori_loop(early, late, weights, 0)
 
     left_dev = (me_e, lax.rem(me_l + lon - 1, lon))
     right_dev = (me_e, lax.rem(me_l + 1, lon))
@@ -241,13 +237,6 @@
             remote(ref.at[which, pl.ds(HALO, HALO), :], ref.at[which, pl.ds(HALO + cols, HALO), :], left_dev),
             remote(ref.at[which, pl.ds(cols, HALO), :], ref.at[which, pl.ds(0, HALO), :], right_dev),
         )
-
-    w_copies = (
-        remote(wmat.at[:, pl.ds(HALO, HALO), :], wmat.at[:, pl.ds(HALO + cols, HALO), :], left_dev),
-        remote(wmat.at[:, pl.ds(cols, HALO), :], wmat.at[:, pl.ds(0, HALO), :], right_dev),
-    )
-    for copy in w_copies:
-        copy.start()
 
     mine = lanes_of(me_e)
     own_a, own_b, pass_a, pass_b = {}, {}, {}, {}
@@ -280,6 +269,19 @@
         fields[c, pl.ds(HALO, cols), mine] = total
         for copy in [own_a[i, c] for i in range(1, na)] + [own_b[j, c] for j in range(1, nb)]:
             copy.start()
+    lax.fori_loop(late, chunks, weights, 0)
+    for s in range(STEPS):
+        wmat[s, pl.ds(HALO, cols), :] = (
+            wsum[pl.ds(s * cols, cols), :] + wsum[pl.ds(slots_cols + s * cols, cols), :]
+        )
+
+    w_copies = (
+        remote(wmat.at[:, pl.ds(HALO, HALO), :], wmat.at[:, pl.ds(HALO + cols, HALO), :], left_dev),
+        remote(wmat.at[:, pl.ds(cols, HALO), :], wmat.at[:, pl.ds(0, HALO), :], right_dev),
+    )
+    for copy in w_copies:
+        copy.start()
+
     load_r.wait()
     for c in range(3):
         for j in range(1, nb):
@@ -302,26 +304,33 @@
     for group in (pass_a, pass_b):
         for copy in group.values():
             copy.wait_send()
+    wide = fields.shape[1]
+    every = range(0, wide, 8)
+
+    def forward(source, target, n, blocks):
+        linear_step(source, target, 1.0, consts, blocks)
+        for start in blocks:
+            heights[n, pl.ds(start, 8), :] = target[0, pl.ds(start, 8), :]
+
+    inside = [range(HALO + 8 * (n + 1), wide - HALO - 8 * (n + 1), 8) for n in range(STEPS)]
+    outer = [[start for start in every if start not in inside[n]] for n in range(STEPS)]
+    buffers = (fields, other, fields, other)
+    for n in range(STEPS):
+        forward(buffers[n], buffers[n + 1], n, inside[n])
     for copy in f_copies:
         copy.wait()
-
-    def forward(source, target, n):
-        linear_step(source, target, 1.0, consts)
-        heights[n] = target[0]
-
-    forward(fields, other, 0)
-    forward(other, fields, 1)
-    forward(fields, other, 2)
+    for n in range(STEPS):
+        forward(buffers[n], buffers[n + 1], n, outer[n])
     for copy in w_copies:
         copy.wait()
     fields[0] = wmat[2] * heights[2]
     fields[1] = jnp.zeros_like(fields[1])
     fields[2] = jnp.zeros_like(fields[2])
-    linear_step(fields, other, -1.0, consts)
+    linear_step(fields, other, -1.0, consts, every)
     other[0] += wmat[1] * heights[1]
-    linear_step(other, fields, -1.0, consts)
+    linear_step(other, fields, -1.0, consts, every)
     fields[0] += wmat[0] * heights[0]
-    linear_step(fields, other, -1.0, consts)
+    linear_step(fields, other, -1.0, consts, every)
 
     for m in range(members):
         total = None

time: 43.8 us -> 42.3 us (0.966)
  Pallas kernels: 39.2 us -> 37.7 us
    pallas_call x1, Pallas kernels: 39.2 us -> 37.7 us  [body(): pl.pallas_call(functools.partial(kernel, ens, lon), out_shape=(jax.ShapeD...]
where the time goes in v3:
time: 42.3 us; the launch traced here: 42.1 us
  Pallas kernels  37.7 us (89%)
  other arithmetic  3.7 us (9%)
  between operations  0.68 us (2%)
    pallas_call x1, Pallas kernels, body(): pl.pallas_call(functools.partial(kernel, ens, lon), out_shape=(jax.ShapeD...  37.7 us
    transpose x1, other arithmetic, body(): return tuple(map(flip, (control_new, residual_new, direction_new)))  2.17 us
    add x1, other arithmetic, body(): control_new = control + step_size * direction  1.54 us

profile of v3, /device:TPU:0, one launch (start us, length us, event | category | flops | bytes accessed | tf_op | source)
XLA Modules:
  0.0 42.1 jit_solution(3214842533975065316)
XLA Ops:
  0.6 0.0 copy-start
  0.6 0.0 copy-start.1
  0.7 0.0 copy-start.2
  0.7 37.7 %shard_map.112 = (f32[2,64,1024]{2,1,0:T(8,128)}, f32[1,1024]{1,0:T(1,128)}, f32[1,1024]{1,0:T(1,128)}) custom-call(f32[2,64,1024]{2,1,0:T(8,128)} %bitcast.15, f32[2,64,1024]{2,1,0:T(8,128)} %bitcast.16, bf16[2,3,64,1024]{3,2,1,0:T(8,128)(2,1)} %bitcast.17, f32[1024,1024]{1,0:T(8,128)} %localize_hbm.1, s32[1,4096]{1,0:T(1,128)} %bitcast.18, ...), custom_call_target="tpu_custom_call" | custom-call | tf_op jit(solution)/shard_map/pallas_call | solution.py:414
  38.4 0.0 copy-done
  38.4 0.0 copy-done.1
  38.4 2.2 %add_bitcast_fusion = (f32[2,1024,64]{1,2,0:T(8,128)}, f32[2,1024,64]{1,2,0:T(8,128)}) fusion(f32[1024]{0:T(1024)} %bitcast.23, f32[2,64,1024]{2,1,0:T(8,128)} %get-tuple-element.7, f32[1024]{0:T(1024)} %bitcast.21, f32[2,1024,64]{1,2,0:T(8,128)S(1)} %copy-done.1, f32[2,1024,64]{1,2,0:T(8,128)S(1)} %copy-done), kind=kLoop, calls=%fused_computation | loop fusion | flops 524288 | bytes 2629632 | tf_op jit(solution)/shard_map/transpose | solution.py:451
  40.6 0.0 copy-done.2
  40.6 1.5 %multiply_add_fusion = f32[2,1024,64]{1,2,0:T(8,128)} fusion(f32[2,1024,64]{1,2,0:T(8,128)S(1)} %copy-done.2, f32[2,1024,64]{1,2,0:T(8,128)S(1)} %copy-done, f32[1024]{0:T(1024)} %bitcast.22), kind=kLoop, calls=%fused_computation.2 | loop fusion | flops 262144 | bytes 1576960 | tf_op jit(solution)/shard_map/add | solution.py:448
Async XLA Ops:
  0.6 37.8 %copy-start = (f32[2,1024,64]{1,2,0:T(8,128)S(1)}, f32[2,1024,64]{1,2,0:T(8,128)}, u32[]{:S(2)}) copy-start(f32[2,1024,64]{1,2,0:T(8,128)} %param.11) | copy-start | bytes 1572868
  0.6 37.8 %copy-start.1 = (f32[2,1024,64]{1,2,0:T(8,128)S(1)}, f32[2,1024,64]{1,2,0:T(8,128)}, u32[]{:S(2)}) copy-start(f32[2,1024,64]{1,2,0:T(8,128)} %param.10) | copy-start | bytes 1572868
  0.7 40.0 %copy-start.2 = (f32[2,1024,64]{1,2,0:T(8,128)S(1)}, f32[2,1024,64]{1,2,0:T(8,128)}, u32[]{:S(2)}) copy-start(f32[2,1024,64]{1,2,0:T(8,128)} %param.9) | copy-start | bytes 1572868
